TPU v7x, 32 devices: a whole 2x2x4 slice. The times are simulated.
32 devices in a mesh: role: 2 (over x), dp: 4 (over y, core), ctx: 4 (over z).
Axes of the slice: x: 2, y: 2, z: 4, core: 2. Of those that a mesh axis runs over, the one named last changes fastest.
Arguments:
- teacher_states: bfloat16 [4, 512, 5120], P('dp', 'ctx'), may hold values from -50 to 50
- student_states: bfloat16 [4, 512, 3584], P('dp', 'ctx'), may hold values from -50 to 50
- teacher_gain: float32 [5120], replicated, may hold values from 0.25 to 1.75
- student_gain: float32 [3584], replicated, may hold values from 0.25 to 1.75
- mentor_output_weights: bfloat16 [4, 5120, 2048], P(None, None, 'ctx'), may hold values from -2 to 2
- student_heads: bfloat16 [4, 3584, 2048], P(None, None, 'ctx'), may hold values from -2 to 2
- segments: int32 [4, 512], P('dp', 'ctx'), may hold values from 0 to 7, never falling along the last dimension, each value on 1 to 256 neighbouring positions
- targets: int32 [4, 512, 4], P('dp', 'ctx'), may hold values from 0 to 2047
Outputs:
- grad_heads: float32 [4, 3584, 2048], P(None, ('role', 'dp'), 'ctx')
- frame_terms: float32 [2, 4, 512, 4], P('role', 'dp', 'ctx')
All inputs are finite; a program needn't handle non-finite values.
Results may differ from a plain program's by a relative error of at most 0.0048.
Values may be sent and summed in bfloat16 or wider, within the bound.
A program may use at most 192 MiB of HBM per device.

v0:
```python
import jax
import jax.numpy as jnp
from jax import lax
from jax.sharding import PartitionSpec as P

QUANTIZER_TOTAL = 4
MBATCH = 4
epsilon = 1e-06
sharpness_divisor = 2.0
blend_ratio = 0.5


def shifted(value, axis, steps):
    count = lax.axis_size(axis)
    initial, last = (max(0, -steps), min(count, count - steps))
    return lax.ppermute(value, axis, [(source, source + steps) for source in range(initial, last)])


def normalize(states, gain):
    values = states.astype(jnp.float32)
    factor = lax.rsqrt(jnp.mean(values * values, axis=-1, keepdims=True) + epsilon)
    return (values * factor * gain).astype(jnp.bfloat16)


def on_device(
    teacher_states,
    student_states,
    teacher_gain,
    student_gain,
    mentor_output_weights,
    student_heads,
    segments,
    targets,
):
    columns = mentor_output_weights.shape[2]
    ctx_count = lax.axis_size("ctx")
    ctx_rank = lax.axis_index("ctx")
    col_start = ctx_rank * columns
    rows_here = teacher_states.shape[1]
    batch_rows = rows_here // MBATCH
    group_rows = batch_rows * ctx_count
    all_segments, all_targets = (
        lax.all_gather(segments, "ctx", axis=1, tiled=True),
        lax.all_gather(targets, "ctx", axis=1, tiled=True),
    )
    length = all_segments.shape[1]
    documents = 2 * ctx_count
    members = (all_segments[0][None, :] == jnp.arange(documents, dtype=jnp.int32)[:, None]).astype(
        jnp.float32
    )
    counts = jnp.sum(members, axis=1)
    row_sizes = jnp.dot(counts, members, precision=lax.Precision.HIGHEST)
    weights = length / (documents * row_sizes)
    own_targets = all_targets[0] - col_start
    is_teacher = lax.axis_index("role") == 0
    positions = jnp.arange(columns)

    def per_batch(values, batch_index):
        trailing = values.shape[1:]
        return values.reshape((ctx_count, MBATCH, batch_rows) + trailing)[:, batch_index].reshape(
            (group_rows,) + trailing
        )

    gradient = jnp.zeros((QUANTIZER_TOTAL, student_heads.shape[1], columns), jnp.float32)
    frame_parts = []
    blocks = []
    teacher_parts = []
    for batch_index in range(MBATCH):
        teacher_local_rows = normalize(
            teacher_states[0, batch_index * batch_rows : (batch_index + 1) * batch_rows],
            teacher_gain,
        )
        scaled = (
            lax.cond(
                is_teacher,
                lambda piece: jnp.einsum(
                    "rd,qdc->rqc", piece, mentor_output_weights, preferred_element_type=jnp.float32
                ),
                lambda piece: jnp.zeros((piece.shape[0], QUANTIZER_TOTAL, columns), jnp.float32),
                lax.all_gather(teacher_local_rows, "ctx", axis=0, tiled=True),
            )
            / sharpness_divisor
        )
        teacher_local_peak = jnp.max(scaled, axis=2)
        teacher_largest_activation = lax.pmax(teacher_local_peak, "ctx")
        totals = lax.psum(
            jnp.sum(jnp.exp(scaled - teacher_largest_activation[:, :, None]), axis=2), "ctx"
        )
        log_probs = scaled - (teacher_largest_activation + jnp.log(totals))[:, :, None]
        teacher_hits = positions[None, None, :] == per_batch(own_targets, batch_index)[:, :, None]
        picked = -jnp.sum(jnp.where(teacher_hits, log_probs, 0.0), axis=2)
        teacher_terms = lax.psum_scatter(picked, "ctx", scatter_dimension=0, tiled=True)
        block = log_probs.astype(jnp.bfloat16)
        blocks.append(block)
        teacher_parts.append(teacher_terms)
    arrived = shifted(jnp.stack(blocks), "role", 1)
    for batch_index in range(MBATCH):
        received = arrived[batch_index]
        student_gradient = gradient
        local_rows = normalize(
            student_states[0, batch_index * batch_rows : (batch_index + 1) * batch_rows],
            student_gain,
        )
        gathered = lax.all_gather(local_rows, "ctx", axis=0, tiled=True)
        raw_activation_grid = lax.cond(
            is_teacher,
            lambda rows: jnp.zeros((rows.shape[0], QUANTIZER_TOTAL, columns), jnp.float32),
            lambda rows: jnp.einsum(
                "rd,qdc->rqc", rows, student_heads, preferred_element_type=jnp.float32
            ),
            gathered,
        )
        local_peak = jnp.max(raw_activation_grid, axis=2)
        largest_activation = lax.pmax(local_peak, "ctx")
        centered_activations = raw_activation_grid - largest_activation[:, :, None]
        plain, warmed_totals = lax.psum(
            (
                jnp.sum(jnp.exp(centered_activations), axis=2),
                jnp.sum(jnp.exp(centered_activations / sharpness_divisor), axis=2),
            ),
            "ctx",
        )
        untempered_logdensity = (
            raw_activation_grid - (largest_activation + jnp.log(plain))[:, :, None]
        )
        warmed_logdensity = (
            raw_activation_grid / sharpness_divisor
            - (largest_activation / sharpness_divisor + jnp.log(warmed_totals))[:, :, None]
        )
        teacher_logp = received.astype(jnp.float32)
        mentor_distribution = jnp.exp(teacher_logp)
        hits = (positions[None, None, :] == per_batch(own_targets, batch_index)[:, :, None]).astype(
            jnp.float32
        )
        kullback_gap = jnp.sum(mentor_distribution * (teacher_logp - warmed_logdensity), axis=2)
        mismatch_penalty = -jnp.sum(hits * untempered_logdensity, axis=2)
        loss_values = (
            blend_ratio * sharpness_divisor * sharpness_divisor * kullback_gap
            + (1.0 - blend_ratio) * mismatch_penalty
        )
        terms = lax.psum_scatter(loss_values, "ctx", scatter_dimension=0, tiled=True)
        gradient_scaling = per_batch(weights, batch_index)[:, None, None] * (
            blend_ratio * sharpness_divisor * (jnp.exp(warmed_logdensity) - mentor_distribution)
            + (1.0 - blend_ratio) * (jnp.exp(untempered_logdensity) - hits)
        )
        gradient_scaling = gradient_scaling.astype(jnp.bfloat16)
        student_gradient = lax.cond(
            is_teacher,
            lambda total: total,
            lambda total: total
            + jnp.einsum(
                "rd,rqc->qdc", gathered, gradient_scaling, preferred_element_type=jnp.float32
            ),
            student_gradient,
        )
        gradient = student_gradient
        frame_parts.append(jnp.where(is_teacher, teacher_parts[batch_index], terms))
    shares = lax.psum_scatter(gradient, ("role", "dp"), scatter_dimension=1, tiled=True)
    frame_terms = jnp.concatenate(frame_parts, axis=0).reshape(1, 1, rows_here, QUANTIZER_TOTAL)
    return (shares, frame_terms)


def solution(mesh):
    return jax.shard_map(
        on_device,
        mesh=mesh,
        in_specs=(
            P("dp", "ctx", None),
            P("dp", "ctx", None),
            P(),
            P(),
            P(None, None, "ctx"),
            P(None, None, "ctx"),
            P("dp", "ctx"),
            P("dp", "ctx", None),
        ),
        out_specs=(P(None, ("role", "dp"), "ctx"), P("role", "dp", "ctx", None)),
        check_vma=False,
    )
```

profile of v0, /device:TPU:0, one launch (start us, length us, event | category | flops | bytes accessed | tf_op | source)
XLA Modules:
  0.0 620.6 jit_solution(17266748540502973690)
XLA Ops:
  16.9 35.9 %all_gather.38 = bf16[128,3584]{1,0:T(8,128)(2,1)} all-gather(bf16[32,3584]{1,0:T(8,128)(2,1)S(1)} %get-tuple-element.195), channel_id=1, replica_groups=mesh['role'=2,'dp'=4,'ctx'=4] {'ctx'}, dimensions={0}, use_global_device_ids=true | all-gather | bytes 1146880 | tf_op jit(solution)/shard_map/all_gather | solution.py:104
  52.7 24.2 %all_gather.31 = bf16[128,3584]{1,0:T(8,128)(2,1)} all-gather(bf16[32,3584]{1,0:T(8,128)(2,1)S(1)} %get-tuple-element.196), channel_id=1, replica_groups=mesh['role'=2,'dp'=4,'ctx'=4] {'ctx'}, dimensions={0}, use_global_device_ids=true | all-gather | bytes 1146880 | tf_op jit(solution)/shard_map/all_gather | solution.py:104
  79.2 32.3 %all_gather.37 = bf16[128,3584]{1,0:T(8,128)(2,1)} all-gather(bf16[32,3584]{1,0:T(8,128)(2,1)S(1)} %get-tuple-element.194), channel_id=1, replica_groups=mesh['role'=2,'dp'=4,'ctx'=4] {'ctx'}, dimensions={0}, use_global_device_ids=true | all-gather | bytes 1146880 | tf_op jit(solution)/shard_map/all_gather | solution.py:104
  113.2 31.1 %all_gather.39 = bf16[128,3584]{1,0:T(8,128)(2,1)} all-gather(bf16[32,3584]{1,0:T(8,128)(2,1)S(1)} %get-tuple-element.193), channel_id=1, replica_groups=mesh['role'=2,'dp'=4,'ctx'=4] {'ctx'}, dimensions={0}, use_global_device_ids=true | all-gather | bytes 1146880 | tf_op jit(solution)/shard_map/all_gather | solution.py:104
  144.9 12.5 %all_gather.36 = s32[1,512,4]{1,2,0:T(4,128)S(1)} all-gather(s32[1,128,4]{1,2,0:T(4,128)S(1)} %copy-done.6), channel_id=1, replica_groups=mesh['role'=2,'dp'=4,'ctx'=4] {'ctx'}, dimensions={1}, use_global_device_ids=true | all-gather | bytes 10240 | tf_op jit(solution)/shard_map/all_gather | solution.py:44
  158.0 13.0 %conditional.14 = (f32[128,4,512]{0,2,1:T(8,128)S(1)}) conditional(s32[]{:T(128)} %convert_element_type.149, () %tuple.84, (bf16[128,5120]{1,0:T(8,128)(2,1)}, bf16[4,5120,512]{2,1,0:T(8,128)(2,1)}) %tuple.85), branch_computations={%region_16.17_spmd, %region_17.18_spmd} | conditional | flops 2684354560 | bytes 23330824 | solution.py:74
  158.1 12.8 %fusion.4 = f32[128,4,512]{0,2,1:T(8,128)S(1)} fusion(bf16[4,5120,512]{2,1,0:T(8,128)(2,1)} %get-tuple-element.93, bf16[128,5120]{1,0:T(8,128)(2,1)} %get-tuple-element.92), kind=kOutput, calls=%fused_computation.4 | convolution fusion | flops 2684354560 | bytes 23330816 | tf_op jit(solution)/shard_map/cond | solution.py:74
  171.0 13.9 %conditional.15 = (f32[128,4,512]{0,2,1:T(8,128)}) conditional(s32[]{:T(128)} %convert_element_type.149, () %tuple.86, (bf16[128,5120]{1,0:T(8,128)(2,1)}, bf16[4,5120,512]{2,1,0:T(8,128)(2,1)}) %tuple.87), branch_computations={%region_23.24_spmd, %region_24.25_spmd} | conditional | flops 2684354560 | bytes 23330824 | solution.py:74
  171.0 13.8 %fusion.6 = f32[128,4,512]{0,2,1:T(8,128)} fusion(bf16[4,5120,512]{2,1,0:T(8,128)(2,1)} %get-tuple-element.95, bf16[128,5120]{1,0:T(8,128)(2,1)} %get-tuple-element.94), kind=kOutput, calls=%fused_computation.6 | convolution fusion | flops 2684354560 | bytes 23330816 | tf_op jit(solution)/shard_map/cond | solution.py:74
  184.9 12.9 %conditional.16 = (f32[128,4,512]{0,2,1:T(8,128)S(1)}) conditional(s32[]{:T(128)} %convert_element_type.149, () %tuple.88, (bf16[128,5120]{1,0:T(8,128)(2,1)}, bf16[4,5120,512]{2,1,0:T(8,128)(2,1)}) %tuple.89), branch_computations={%region_30.31_spmd, %region_31.32_spmd} | conditional | flops 2684354560 | bytes 23330824 | solution.py:74
  184.9 12.7 %fusion.8 = f32[128,4,512]{0,2,1:T(8,128)S(1)} fusion(bf16[4,5120,512]{2,1,0:T(8,128)(2,1)} %get-tuple-element.102, bf16[128,5120]{1,0:T(8,128)(2,1)} %get-tuple-element.100), kind=kOutput, calls=%fused_computation.8 | convolution fusion | flops 2684354560 | bytes 23330816 | tf_op jit(solution)/shard_map/cond | solution.py:74
  200.3 12.8 %conditional.13 = (f32[128,4,512]{0,2,1:T(8,128)S(1)}) conditional(s32[]{:T(128)} %convert_element_type.149, () %tuple.82, (bf16[128,5120]{1,0:T(8,128)(2,1)}, bf16[4,5120,512]{2,1,0:T(8,128)(2,1)}) %tuple.83), branch_computations={%region_9.10_spmd, %region_10.11_spmd} | conditional | flops 2684354560 | bytes 23330824 | solution.py:74
  200.3 12.8 %fusion.2 = f32[128,4,512]{0,2,1:T(8,128)S(1)} fusion(bf16[4,5120,512]{2,1,0:T(8,128)(2,1)} %get-tuple-element.90, bf16[128,5120]{1,0:T(8,128)(2,1)} %get-tuple-element.85), kind=kOutput, calls=%fused_computation.2 | convolution fusion | flops 2684354560 | bytes 23330816 | tf_op jit(solution)/shard_map/cond | solution.py:74
  214.2 17.6 %all-reduce.1 = (f32[128,4]{0,1:T(4,128)S(1)}, f32[128,4]{0,1:T(4,128)S(1)}, f32[128,4]{0,1:T(4,128)S(1)}, f32[128,4]{0,1:T(4,128)S(1)}, f32[128,4]{0,1:T(4,128)...) all-reduce(f32[128,4]{0,1:T(4,128)S(1)} %reduce_max.72, ...), channel_id=1, replica_groups=mesh['role'=2,'dp'=4,'ctx'=4] {'ctx'}, use_global_device_ids=true, to_apply=%region_5.0 | all-reduce | flops 4096 | bytes 32768 | tf_op jit(solution)/shard_map/pmax | solution.py:114
  239.9 15.7 %all-reduce = (f32[128,4]{0,1:T(4,128)S(1)}, f32[128,4]{0,1:T(4,128)S(1)}, f32[128,4]{0,1:T(4,128)S(1)}, f32[128,4]{0,1:T(4,128)S(1)}, f32[128,4]{0,1:T(4,128)S(...) all-reduce(f32[128,4]{0,1:T(4,128)S(1)} %get-tuple-element.141, ...), channel_id=1, replica_groups=mesh['role'=2,'dp'=4,'ctx'=4] {'ctx'}, use_global_device_ids=true, to_apply=%region_37.38 | all-reduce | flops 6144 | bytes 49152 | tf_op jit(solution)/shard_map/psum | solution.py:116
  279.3 17.3 %collective-permute-done = bf16[4,128,4,512]{1,3,2,0:T(8,128)(2,1)} collective-permute-done((bf16[4,128,4,512]{1,3,2,0:T(8,128)(2,1)}, bf16[4,128,4,512]{1,3,2,0:T(8,128)(2,1)}, u32[]{:S(2)}, u32[]{:S(2)}) %collective-permute-start) | collective-permute-done | bytes 2097184 | tf_op jit(solution)/shard_map/ppermute | solution.py:16
  310.1 13.5 %conditional.20 = (f32[4,3584,512]{1,2,0:T(8,128)}) conditional(s32[]{:T(128)} %convert_element_type.149, (bf16[128,4,512]{0,2,1:T(8,128)(2,1)S(1)}, bf16[128,3584]{1,0:T(8,128)(2,1)}) %tuple.96, () %tuple.97), branch_computations={%region_65.66_spmd, %region_66.67_spmd} | conditional | flops 1879048192 | bytes 30801928 | solution.py:147
  310.1 13.4 %broadcast_in_dim.6 = f32[4,3584,512]{1,2,0:T(8,128)} broadcast(f32[]{:T(128)} %constant.65.clone), dimensions={} | broadcast | bytes 29360132 | tf_op jit(solution)/shard_map/broadcast_in_dim | solution.py:64
  324.8 27.6 %copy.77 = f32[4,3584,512]{2,1,0:T(8,128)} copy(f32[4,3584,512]{1,2,0:T(8,128)} %get-tuple-element.228) | data formatting | bytes 58720256 | tf_op jit(solution)/shard_map/cond | solution.py:147
  355.6 16.0 %reduce-scatter.42.cloned.1.call-done = f32[32,4]{1,0:T(8,128)} async-done(((f32[128,4]{1,0:T(8,128)}), f32[32,4]{1,0:T(8,128)}) %reduce-scatter.42.cloned.1.call-update) | async-done | bytes 528
  372.5 18.8 %reduce-scatter.38.cloned.1.call-done = f32[32,4]{1,0:T(8,128)} async-done(((f32[128,4]{1,0:T(8,128)}), f32[32,4]{1,0:T(8,128)}) %reduce-scatter.38.cloned.1.call-update) | async-done | bytes 528
  392.0 18.9 %reduce-scatter.34.cloned.1.call-done = f32[32,4]{1,0:T(8,128)} async-done(((f32[128,4]{1,0:T(8,128)}), f32[32,4]{1,0:T(8,128)}) %reduce-scatter.34.cloned.1.call-update) | async-done | bytes 528
  411.8 18.8 %reduce-scatter.30.cloned.1.call-done = f32[32,4]{1,0:T(8,128)} async-done(((f32[128,4]{1,0:T(8,128)}), f32[32,4]{1,0:T(8,128)}) %reduce-scatter.30.cloned.1.call-update) | async-done | bytes 528
  432.0 181.9 %reduce-scatter.26.cloned.1.call-done = f32[4,448,512]{2,1,0:T(8,128)} async-done(((f32[4,3584,512]{2,1,0:T(8,128)}), f32[4,448,512]{2,1,0:T(8,128)}) %reduce-scatter.26.cloned.1.call-update) | async-done | bytes 3670032 | tf_op jit(solution)/shard_map/reduce_scatter | solution.py:158
  (152 shorter events, 71.9 us)
Async XLA Ops:
  7.2 150.8 %all-gather.7.cloned.1.call-start = ((), (), s32[]{:S(2)}) async-start(), calls=%async_computation.10 | async-start | bytes 1638400 | tf_op jit(solution)/shard_map/all_gather | solution.py:80
  11.5 159.4 %all-gather.9.cloned.1.call-start = ((), (), s32[]{:S(2)}) async-start(), calls=%async_computation.11 | async-start | bytes 1638400 | tf_op jit(solution)/shard_map/all_gather | solution.py:80
  12.3 172.6 %all-gather.11.cloned.1.call-start = ((), (), s32[]{:S(2)}) async-start(), calls=%async_computation.12 | async-start | bytes 1638400 | tf_op jit(solution)/shard_map/all_gather | solution.py:80
  13.0 187.3 %all-gather.5.cloned.1.call-start = ((), (), s32[]{:S(2)}) async-start(), calls=%async_computation.9 | async-start | bytes 1638400 | tf_op jit(solution)/shard_map/all_gather | solution.py:80
  13.6 338.8 %reduce-scatter.28.cloned.1.call-start = ((), (), s32[]{:S(2)}) async-start(), calls=%async_computation.14 | async-start | bytes 81920
  111.7 33.3 %copy-start.6 = (s32[1,128,4]{1,2,0:T(4,128)S(1)}, s32[1,128,4]{1,2,0:T(4,128)}, u32[]{:S(2)}) copy-start(s32[1,128,4]{1,2,0:T(4,128)} %param.39) | copy-start | bytes 6148
  171.0 29.2 %copy-start.1 = (f32[128,4,512]{0,2,1:T(8,128)}, f32[128,4,512]{0,2,1:T(8,128)S(1)}, u32[]{:S(2)}) copy-start(f32[128,4,512]{0,2,1:T(8,128)S(1)} %get-tuple-element.123) | copy-start | bytes 3145732
  197.8 1.0 copy-start.2
  200.3 38.7 %copy-start = (f32[128,4,512]{0,2,1:T(8,128)S(1)}, f32[128,4,512]{0,2,1:T(8,128)}, u32[]{:S(2)}) copy-start(f32[128,4,512]{0,2,1:T(8,128)} %copy.68) | copy-start | bytes 3145732
  213.1 1.0 copy-start.3
  213.1 52.7 %copy-start.7 = (s32[1,128]{1,0:T(1,128)S(1)}, s32[1,128]{1,0:T(1,128)}, u32[]{:S(2)}) copy-start(s32[1,128]{1,0:T(1,128)} %param.38) | copy-start | bytes 1540
  263.2 33.4 %collective-permute-start = (bf16[4,128,4,512]{1,3,2,0:T(8,128)(2,1)}, bf16[4,128,4,512]{1,3,2,0:T(8,128)(2,1)}, u32[]{:S(2)}, u32[]{:S(2)}) collective-permute-start(bf16[4,128,4,512]{1,3,2,0:T(8,128)(2,1)} %pad_maximum_fusion), channel_id=1, source_target_pairs={{0,16},{1,17},{2,18},{3,19},{4,20},{5,21},{6,22},{7,23},{8,24},{9,... | collective-permute-start | bytes 6291464 | tf_op jit(solution)/shard_map/ppermute | solution.py:16
  276.2 77.0 %reduce-scatter.40.cloned.1.call-start = ((), (), s32[]{:S(2)}) async-start(), calls=%async_computation.20 | async-start | bytes 81920
  277.1 76.9 %reduce-scatter.36.cloned.1.call-start = ((), (), s32[]{:S(2)}) async-start(), calls=%async_computation.18 | async-start | bytes 81920
  278.0 76.8 %reduce-scatter.32.cloned.1.call-start = ((), (), s32[]{:S(2)}) async-start(), calls=%async_computation.16 | async-start | bytes 81920
  279.2 92.5 %reduce-scatter.42.cloned.1.call-start = ((), (), s32[]{:S(2)}) async-start(), calls=%async_computation.21 | async-start | bytes 81920
  301.0 90.2 %reduce-scatter.38.cloned.1.call-start = ((), (), s32[]{:S(2)}) async-start(), calls=%async_computation.19 | async-start | bytes 81920
  301.8 109.1 %reduce-scatter.34.cloned.1.call-start = ((), (), s32[]{:S(2)}) async-start(), calls=%async_computation.17 | async-start | bytes 81920
  302.7 127.9 %reduce-scatter.30.cloned.1.call-start = ((), (), s32[]{:S(2)}) async-start(), calls=%async_computation.15 | async-start | bytes 81920
  303.5 310.5 %reduce-scatter.26.cloned.1.call-start = ((), (), s32[]{:S(2)}) async-start(), calls=%async_computation.13 | async-start | bytes 33030144 | tf_op jit(solution)/shard_map/reduce_scatter | solution.py:158
  310.1 13.5 %copy-start.5 = (bf16[128,4,512]{0,2,1:T(8,128)(2,1)S(1)}, bf16[128,4,512]{0,2,1:T(8,128)(2,1)}, u32[]{:S(2)}) copy-start(bf16[128,4,512]{0,2,1:T(8,128)(2,1)} %get-tuple-element.180) | copy-start | bytes 1572868
  323.6 1.0 copy-start.4
Sparse Core Ops, SparseCore 0:
  11.7 49.2 all-gather.6
  62.5 45.3 all-gather.8
  109.5 42.2 all-gather.10
  153.2 34.2 all-gather.4
  276.3 16.5 reduce-scatter.27
  295.0 17.4 reduce-scatter.39
  314.7 17.4 reduce-scatter.35
  334.5 17.4 reduce-scatter.31
  354.2 17.4 reduce-scatter.41
  373.8 17.4 reduce-scatter.37
  393.5 17.4 reduce-scatter.33
  413.1 17.4 reduce-scatter.29
  434.7 179.1 reduce-scatter.25
where the time goes:
time: 630 us; the launch traced here: 621 us
  waiting for transfers between devices  274 us (43%)
  blocking collectives  179 us (28%)
  local copies, waits for them, and re-layouts  61.1 us (10%)
  matrix products  52.3 us (8%)
  other arithmetic  36 us (6%)
  between operations  14.5 us (2%)
    reduce_scatter x1, waiting for transfers between devices, on_device(): lax.psum_scatter(gradient, ('role', 'dp'), scatter_dimension=1, tiled=True)  182 us
    all_gather x4, blocking collectives, on_device(): gathered = lax.all_gather(local_rows, 'ctx', axis=0, tiled=True)  124 us
    unnamed x21, waiting for transfers between devices  74.6 us
    cond x4, matrix products, on_device(): lax.cond(is_teacher, lambda piece: jnp.einsum('rd,qdc->rqc', piece, mento...  52.2 us
    cond x1, local copies, waits for them, and re-layouts, on_device(): lax.cond(is_teacher, lambda total: total, lambda total: total + jnp.einsu...  27.6 us
    pmax x1, blocking collectives, on_device(): largest_activation = lax.pmax(local_peak, 'ctx')  17.6 us
    ppermute x1, waiting for transfers between devices, shifted(): lax.ppermute(value, axis, [(source, source + steps) for source in range(i...  17.3 us
    psum x1, blocking collectives, on_device(): lax.psum((jnp.sum(jnp.exp(centered_activations), axis=2), jnp.sum(jnp.exp...  15.7 us
  transfers between devices with their start and end apart: 14, of which 6 were waited for; matrix products, arithmetic and copies ran while one was open for 18% of the time, Pallas kernels for 0%

commit v1 on v0

--- a/solution.py
+++ b/solution.py
@@ -101,7 +101,13 @@
             student_states[0, batch_index * batch_rows : (batch_index + 1) * batch_rows],
             student_gain,
         )
-        gathered = lax.all_gather(local_rows, "ctx", axis=0, tiled=True)
+        peers = lax.axis_size("ctx")
+        held, pieces = (local_rows, [local_rows])
+        for _ in range(peers - 1):
+            held = lax.ppermute(held, "ctx", [(i, (i + 1) % peers) for i in range(peers)])
+            pieces.insert(0, held)
+        flat = jnp.concatenate(pieces, axis=0)
+        gathered = jnp.roll(flat, (lax.axis_index("ctx") + 1) * local_rows.shape[0], axis=0)
         raw_activation_grid = lax.cond(
             is_teacher,
             lambda rows: jnp.zeros((rows.shape[0], QUANTIZER_TOTAL, columns), jnp.float32),

time: 630 us -> 608 us (0.965)
  blocking collectives: 179 us -> 87.2 us
  waiting for transfers between devices: 274 us -> 322 us
  starting transfers between devices: 3.57 us -> 19.5 us
    all_gather x4 -> x0, blocking collectives: 124 us -> none  [on_device(): gathered = lax.all_gather(local_rows, 'ctx', axis=0, tiled=True)]
    ppermute x0 -> x12, waiting for transfers between devices: none -> 46.5 us  [on_device(): lax.ppermute(held, 'ctx', [(i, (i + 1) % peers) for i in range(peers)])]
    all_gather x1, blocking collectives: 12.5 us -> 45.1 us  [on_device(): lax.all_gather(targets, 'ctx', axis=1, tiled=True)]
    ppermute x0 -> x12, starting transfers between devices: none -> 16.1 us  [on_device(): lax.ppermute(held, 'ctx', [(i, (i + 1) % peers) for i in range(peers)])]
    concatenate x0 -> x4, other arithmetic: none -> 13.5 us  [on_device(): jnp.roll(flat, (lax.axis_index('ctx') + 1) * local_rows.shape[0], axis=0)]
    unnamed x21, waiting for transfers between devices: 74.6 us -> 68.1 us
    unnamed x32 -> x56, local copies, waits for them, and re-layouts: 15.2 us -> 15.5 us
  transfers between devices with their start and end apart: 14 -> 26, of which waited for: 6 -> 13; matrix products, arithmetic and copies ran while one was open for 18% -> 21% of each run, Pallas kernels for 0% -> 0%
where the time goes in v1:
time: 608 us; the launch traced here: 599 us
  waiting for transfers between devices  322 us (53%)
  blocking collectives  87.2 us (14%)
  local copies, waits for them, and re-layouts  61.4 us (10%)
  matrix products  52.1 us (9%)
  other arithmetic  40.5 us (7%)
  starting transfers between devices  19.5 us (3%)
  between operations  14.7 us (2%)
    reduce_scatter x1, waiting for transfers between devices, on_device(): lax.psum_scatter(gradient, ('role', 'dp'), scatter_dimension=1, tiled=True)  182 us
    unnamed x21, waiting for transfers between devices  68.1 us
    cond x4, matrix products, on_device(): lax.cond(is_teacher, lambda piece: jnp.einsum('rd,qdc->rqc', piece, mento...  52 us
    ppermute x12, waiting for transfers between devices, on_device(): lax.ppermute(held, 'ctx', [(i, (i + 1) % peers) for i in range(peers)])  46.5 us
    all_gather x1, blocking collectives, on_device(): lax.all_gather(targets, 'ctx', axis=1, tiled=True)  45.1 us
    cond x1, local copies, waits for them, and re-layouts, on_device(): lax.cond(is_teacher, lambda total: total, lambda total: total + jnp.einsu...  27.6 us
    ppermute x1, waiting for transfers between devices, shifted(): lax.ppermute(value, axis, [(source, source + steps) for source in range(i...  23.3 us
    pmax x1, blocking collectives, on_device(): largest_activation = lax.pmax(local_peak, 'ctx')  16.9 us
  transfers between devices with their start and end apart: 26, of which 13 were waited for; matrix products, arithmetic and copies ran while one was open for 21% of the time, Pallas kernels for 0%

profile of v1, /device:TPU:0, one launch (start us, length us, event | category | flops | bytes accessed | tf_op | source)
XLA Modules:
  0.0 599.0 jit_solution(10661042038938093277)
XLA Ops:
  25.3 45.1 %all_gather.23 = s32[1,512,4]{1,2,0:T(4,128)S(1)} all-gather(s32[1,128,4]{1,2,0:T(4,128)S(1)} %copy-done.18), channel_id=1, replica_groups=mesh['role'=2,'dp'=4,'ctx'=4] {'ctx'}, dimensions={1}, use_global_device_ids=true | all-gather | bytes 10240 | tf_op jit(solution)/shard_map/all_gather | solution.py:44
  75.9 8.5 %collective-permute-done.11 = bf16[32,3584]{1,0:T(8,128)(2,1)} collective-permute-done((bf16[32,3584]{1,0:T(8,128)(2,1)S(1)}, bf16[32,3584]{1,0:T(8,128)(2,1)}, u32[]{:S(2)}, u32[]{:S(2)}) %collective-permute-start.11) | collective-permute-done | bytes 229408 | tf_op jit(solution)/shard_map/ppermute | solution.py:107
  85.5 8.6 %collective-permute-done.8 = bf16[32,3584]{1,0:T(8,128)(2,1)S(1)} collective-permute-done((bf16[32,3584]{1,0:T(8,128)(2,1)S(1)}, bf16[32,3584]{1,0:T(8,128)(2,1)S(1)}, u32[]{:S(2)}, u32[]{:S(2)}) %collective-permute-start.8) | collective-permute-done | bytes 229408 | tf_op jit(solution)/shard_map/ppermute | solution.py:107
  105.7 8.2 %collective-permute-done.6 = bf16[32,3584]{1,0:T(8,128)(2,1)} collective-permute-done((bf16[32,3584]{1,0:T(8,128)(2,1)S(1)}, bf16[32,3584]{1,0:T(8,128)(2,1)}, u32[]{:S(2)}, u32[]{:S(2)}) %collective-permute-start.6) | collective-permute-done | bytes 229408 | tf_op jit(solution)/shard_map/ppermute | solution.py:107
  140.0 13.0 %conditional.14 = (f32[128,4,512]{0,2,1:T(8,128)S(1)}) conditional(s32[]{:T(128)} %convert_element_type.149, () %tuple.85, (bf16[128,5120]{1,0:T(8,128)(2,1)}, bf16[4,5120,512]{2,1,0:T(8,128)(2,1)}) %tuple.86), branch_computations={%region_16.0_spmd, %region_17.0_spmd} | conditional | flops 2684354560 | bytes 23330824 | solution.py:74
  140.3 12.7 %fusion.4 = f32[128,4,512]{0,2,1:T(8,128)S(1)} fusion(bf16[4,5120,512]{2,1,0:T(8,128)(2,1)} %get-tuple-element.94, bf16[128,5120]{1,0:T(8,128)(2,1)} %get-tuple-element.92), kind=kOutput, calls=%fused_computation.4 | convolution fusion | flops 2684354560 | bytes 23330816 | tf_op jit(solution)/shard_map/cond | solution.py:74
  153.0 13.8 %conditional.15 = (f32[128,4,512]{0,2,1:T(8,128)}) conditional(s32[]{:T(128)} %convert_element_type.149, () %tuple.87, (bf16[128,5120]{1,0:T(8,128)(2,1)}, bf16[4,5120,512]{2,1,0:T(8,128)(2,1)}) %tuple.88), branch_computations={%region_23.0_spmd, %region_24.0_spmd} | conditional | flops 2684354560 | bytes 23330824 | solution.py:74
  153.1 13.8 %fusion.6 = f32[128,4,512]{0,2,1:T(8,128)} fusion(bf16[4,5120,512]{2,1,0:T(8,128)(2,1)} %get-tuple-element.96, bf16[128,5120]{1,0:T(8,128)(2,1)} %get-tuple-element.95), kind=kOutput, calls=%fused_computation.6 | convolution fusion | flops 2684354560 | bytes 23330816 | tf_op jit(solution)/shard_map/cond | solution.py:74
  166.8 13.1 %conditional.16 = (f32[128,4,512]{0,2,1:T(8,128)S(1)}) conditional(s32[]{:T(128)} %convert_element_type.149, () %tuple.89, (bf16[128,5120]{1,0:T(8,128)(2,1)}, bf16[4,5120,512]{2,1,0:T(8,128)(2,1)}) %tuple.90), branch_computations={%region_30.0_spmd, %region_31.0_spmd} | conditional | flops 2684354560 | bytes 23330824 | solution.py:74
  166.8 12.7 %fusion.8 = f32[128,4,512]{0,2,1:T(8,128)S(1)} fusion(bf16[4,5120,512]{2,1,0:T(8,128)(2,1)} %get-tuple-element.102, bf16[128,5120]{1,0:T(8,128)(2,1)} %get-tuple-element.97), kind=kOutput, calls=%fused_computation.8 | convolution fusion | flops 2684354560 | bytes 23330816 | tf_op jit(solution)/shard_map/cond | solution.py:74
  185.2 12.8 %conditional.13 = (f32[128,4,512]{0,2,1:T(8,128)S(1)}) conditional(s32[]{:T(128)} %convert_element_type.149, () %tuple.83, (bf16[128,5120]{1,0:T(8,128)(2,1)}, bf16[4,5120,512]{2,1,0:T(8,128)(2,1)}) %tuple.84), branch_computations={%region_9.0_spmd, %region_10.0_spmd} | conditional | flops 2684354560 | bytes 23330824 | solution.py:74
  185.2 12.8 %fusion.2 = f32[128,4,512]{0,2,1:T(8,128)S(1)} fusion(bf16[4,5120,512]{2,1,0:T(8,128)(2,1)} %get-tuple-element.87, bf16[128,5120]{1,0:T(8,128)(2,1)} %get-tuple-element.86), kind=kOutput, calls=%fused_computation.2 | convolution fusion | flops 2684354560 | bytes 23330816 | tf_op jit(solution)/shard_map/cond | solution.py:74
  199.0 16.9 %all-reduce.1 = (f32[128,4]{0,1:T(4,128)S(1)}, f32[128,4]{0,1:T(4,128)S(1)}, f32[128,4]{0,1:T(4,128)S(1)}, f32[128,4]{0,1:T(4,128)S(1)}, f32[128,4]{0,1:T(4,128)...) all-reduce(f32[128,4]{0,1:T(4,128)S(1)} %reduce_max.72, ...), channel_id=1, replica_groups=mesh['role'=2,'dp'=4,'ctx'=4] {'ctx'}, use_global_device_ids=true, to_apply=%region_5.7 | all-reduce | flops 4096 | bytes 32768 | tf_op jit(solution)/shard_map/pmax | solution.py:120
  220.6 15.7 %all-reduce = (f32[128,4]{0,1:T(4,128)S(1)}, f32[128,4]{0,1:T(4,128)S(1)}, f32[128,4]{0,1:T(4,128)S(1)}, f32[128,4]{0,1:T(4,128)S(1)}, f32[128,4]{0,1:T(4,128)S(...) all-reduce(f32[128,4]{0,1:T(4,128)S(1)} %get-tuple-element.142, ...), channel_id=1, replica_groups=mesh['role'=2,'dp'=4,'ctx'=4] {'ctx'}, use_global_device_ids=true, to_apply=%region_37.0 | all-reduce | flops 6144 | bytes 49152 | tf_op jit(solution)/shard_map/psum | solution.py:122
  244.4 9.4 %all_gather.18 = s32[1,512]{1,0:T(1,128)S(1)} all-gather(s32[1,128]{1,0:T(1,128)S(1)} %copy-done.19), channel_id=1, replica_groups=mesh['role'=2,'dp'=4,'ctx'=4] {'ctx'}, dimensions={1}, use_global_device_ids=true | all-gather | bytes 2560 | tf_op jit(solution)/shard_map/all_gather | solution.py:43
  257.8 23.3 %collective-permute-done.3 = bf16[4,128,4,512]{1,3,2,0:T(8,128)(2,1)} collective-permute-done((bf16[4,128,4,512]{1,3,2,0:T(8,128)(2,1)}, bf16[4,128,4,512]{1,3,2,0:T(8,128)(2,1)}, u32[]{:S(2)}, u32[]{:S(2)}) %collective-permute-start.3) | collective-permute-done | bytes 2097184 | tf_op jit(solution)/shard_map/ppermute | solution.py:16
  294.2 13.5 %conditional.20 = (f32[4,3584,512]{1,2,0:T(8,128)}) conditional(s32[]{:T(128)} %convert_element_type.149, (bf16[128,4,512]{0,2,1:T(8,128)(2,1)S(1)}, bf16[128,3584]{1,0:T(8,128)(2,1)}) %tuple.97, () %tuple.98), branch_computations={%region_65.67_spmd, %region_66.68_spmd} | conditional | flops 1879048192 | bytes 30801928 | solution.py:153
  294.3 13.5 %broadcast_in_dim.6 = f32[4,3584,512]{1,2,0:T(8,128)} broadcast(f32[]{:T(128)} %constant.84.clone), dimensions={} | broadcast | bytes 29360132 | tf_op jit(solution)/shard_map/broadcast_in_dim | solution.py:64
  309.3 27.6 %copy.77 = f32[4,3584,512]{2,1,0:T(8,128)} copy(f32[4,3584,512]{1,2,0:T(8,128)} %get-tuple-element.229) | data formatting | bytes 58720256 | tf_op jit(solution)/shard_map/cond | solution.py:153
  340.1 10.1 %reduce-scatter.42.cloned.1.call-done = f32[32,4]{1,0:T(8,128)} async-done(((f32[128,4]{1,0:T(8,128)}), f32[32,4]{1,0:T(8,128)}) %reduce-scatter.42.cloned.1.call-update) | async-done | bytes 528
  351.0 18.7 %reduce-scatter.38.cloned.1.call-done = f32[32,4]{1,0:T(8,128)} async-done(((f32[128,4]{1,0:T(8,128)}), f32[32,4]{1,0:T(8,128)}) %reduce-scatter.38.cloned.1.call-update) | async-done | bytes 528
  370.5 18.9 %reduce-scatter.34.cloned.1.call-done = f32[32,4]{1,0:T(8,128)} async-done(((f32[128,4]{1,0:T(8,128)}), f32[32,4]{1,0:T(8,128)}) %reduce-scatter.34.cloned.1.call-update) | async-done | bytes 528
  390.2 18.8 %reduce-scatter.30.cloned.1.call-done = f32[32,4]{1,0:T(8,128)} async-done(((f32[128,4]{1,0:T(8,128)}), f32[32,4]{1,0:T(8,128)}) %reduce-scatter.30.cloned.1.call-update) | async-done | bytes 528
  410.4 181.8 %reduce-scatter.26.cloned.1.call-done = f32[4,448,512]{2,1,0:T(8,128)} async-done(((f32[4,3584,512]{2,1,0:T(8,128)}), f32[4,448,512]{2,1,0:T(8,128)}) %reduce-scatter.26.cloned.1.call-update) | async-done | bytes 3670032 | tf_op jit(solution)/shard_map/reduce_scatter | solution.py:164
  (200 shorter events, 106.9 us)
Async XLA Ops:
  7.2 132.8 %all-gather.7.cloned.1.call-start = ((), (), s32[]{:S(2)}) async-start(), calls=%async_computation.10 | async-start | bytes 1638400 | tf_op jit(solution)/shard_map/all_gather | solution.py:80
  11.2 141.8 %all-gather.9.cloned.1.call-start = ((), (), s32[]{:S(2)}) async-start(), calls=%async_computation.11 | async-start | bytes 1638400 | tf_op jit(solution)/shard_map/all_gather | solution.py:80
  11.9 154.9 %all-gather.11.cloned.1.call-start = ((), (), s32[]{:S(2)}) async-start(), calls=%async_computation.12 | async-start | bytes 1638400 | tf_op jit(solution)/shard_map/all_gather | solution.py:80
  12.7 172.5 %all-gather.5.cloned.1.call-start = ((), (), s32[]{:S(2)}) async-start(), calls=%async_computation.9 | async-start | bytes 1638400 | tf_op jit(solution)/shard_map/all_gather | solution.py:80
  16.5 54.0 %collective-permute-start.10 = (bf16[32,3584]{1,0:T(8,128)(2,1)S(1)}, bf16[32,3584]{1,0:T(8,128)(2,1)S(1)}, u32[]{:S(2)}, u32[]{:S(2)}) collective-permute-start(bf16[32,3584]{1,0:T(8,128)(2,1)S(1)} %get-tuple-element.194), channel_id=1, source_target_pairs={{0,1},{1,2},{2,3},{3,0},{4,5},{5,6},{6,7},{7,4},{8,9},{9,10},{10,1... | collective-permute-start | bytes 688136 | tf_op jit(solution)/shard_map/ppermute | solution.py:107
  18.0 54.0 %collective-permute-start.7 = (bf16[32,3584]{1,0:T(8,128)(2,1)S(1)}, bf16[32,3584]{1,0:T(8,128)(2,1)S(1)}, u32[]{:S(2)}, u32[]{:S(2)}) collective-permute-start(bf16[32,3584]{1,0:T(8,128)(2,1)S(1)} %get-tuple-element.196), channel_id=1, source_target_pairs={{0,1},{1,2},{2,3},{3,0},{4,5},{5,6},{6,7},{7,4},{8,9},{9,10},{10,1... | collective-permute-start | bytes 688136 | tf_op jit(solution)/shard_map/ppermute | solution.py:107
  19.6 52.5 %collective-permute-start = (bf16[32,3584]{1,0:T(8,128)(2,1)S(1)}, bf16[32,3584]{1,0:T(8,128)(2,1)S(1)}, u32[]{:S(2)}, u32[]{:S(2)}) collective-permute-start(bf16[32,3584]{1,0:T(8,128)(2,1)S(1)} %get-tuple-element.197), channel_id=1, source_target_pairs={{0,1},{1,2},{2,3},{3,0},{4,5},{5,6},{6,7},{7,4},{8,9},{9,10},{10,1... | collective-permute-start | bytes 688136 | tf_op jit(solution)/shard_map/ppermute | solution.py:107
  25.0 48.7 %collective-permute-start.5 = (bf16[32,3584]{1,0:T(8,128)(2,1)S(1)}, bf16[32,3584]{1,0:T(8,128)(2,1)S(1)}, u32[]{:S(2)}, u32[]{:S(2)}) collective-permute-start(bf16[32,3584]{1,0:T(8,128)(2,1)S(1)} %collective-permute-done.4), channel_id=1, source_target_pairs={{0,1},{1,2},{2,3},{3,0},{4,5},{5,6},{6,7},{7,4},{8,9},{9,10},{10,1... | collective-permute-start | bytes 688136 | tf_op jit(solution)/shard_map/ppermute | solution.py:107
  25.2 311.6 %reduce-scatter.28.cloned.1.call-start = ((), (), s32[]{:S(2)}) async-start(), calls=%async_computation.14 | async-start | bytes 81920
  72.0 22.1 %collective-permute-start.8 = (bf16[32,3584]{1,0:T(8,128)(2,1)S(1)}, bf16[32,3584]{1,0:T(8,128)(2,1)S(1)}, u32[]{:S(2)}, u32[]{:S(2)}) collective-permute-start(bf16[32,3584]{1,0:T(8,128)(2,1)S(1)} %collective-permute-done.7), channel_id=1, source_target_pairs={{0,1},{1,2},{2,3},{3,0},{4,5},{5,6},{6,7},{7,4},{8,9},{9,10},{10,1... | collective-permute-start | bytes 688136 | tf_op jit(solution)/shard_map/ppermute | solution.py:107
  72.1 31.8 %collective-permute-start.1 = (bf16[32,3584]{1,0:T(8,128)(2,1)S(1)}, bf16[32,3584]{1,0:T(8,128)(2,1)S(1)}, u32[]{:S(2)}, u32[]{:S(2)}) collective-permute-start(bf16[32,3584]{1,0:T(8,128)(2,1)S(1)} %collective-permute-done), channel_id=1, source_target_pairs={{0,1},{1,2},{2,3},{3,0},{4,5},{5,6},{6,7},{7,4},{8,9},{9,10},{10,1... | collective-permute-start | bytes 688136 | tf_op jit(solution)/shard_map/ppermute | solution.py:107
  73.7 40.2 %collective-permute-start.6 = (bf16[32,3584]{1,0:T(8,128)(2,1)S(1)}, bf16[32,3584]{1,0:T(8,128)(2,1)}, u32[]{:S(2)}, u32[]{:S(2)}) collective-permute-start(bf16[32,3584]{1,0:T(8,128)(2,1)S(1)} %collective-permute-done.5), channel_id=1, source_target_pairs={{0,1},{1,2},{2,3},{3,0},{4,5},{5,6},{6,7},{7,4},{8,9},{9,10},{10,1... | collective-permute-start | bytes 688136 | tf_op jit(solution)/shard_map/ppermute | solution.py:107
  84.4 51.0 %collective-permute-start.12 = (bf16[32,3584]{1,0:T(8,128)(2,1)}, bf16[32,3584]{1,0:T(8,128)(2,1)}, u32[]{:S(2)}, u32[]{:S(2)}) collective-permute-start(bf16[32,3584]{1,0:T(8,128)(2,1)} %collective-permute-done.11), channel_id=1, source_target_pairs={{0,1},{1,2},{2,3},{3,0},{4,5},{5,6},{6,7},{7,4},{8,9},{9,10},{10,1... | collective-permute-start | bytes 688136 | tf_op jit(solution)/shard_map/ppermute | solution.py:107
  94.1 30.7 %collective-permute-start.9 = (bf16[32,3584]{1,0:T(8,128)(2,1)S(1)}, bf16[32,3584]{1,0:T(8,128)(2,1)S(1)}, u32[]{:S(2)}, u32[]{:S(2)}) collective-permute-start(bf16[32,3584]{1,0:T(8,128)(2,1)S(1)} %collective-permute-done.8), channel_id=1, source_target_pairs={{0,1},{1,2},{2,3},{3,0},{4,5},{5,6},{6,7},{7,4},{8,9},{9,10},{10,1... | collective-permute-start | bytes 688136 | tf_op jit(solution)/shard_map/ppermute | solution.py:107
  103.9 24.1 %collective-permute-start.2 = (bf16[32,3584]{1,0:T(8,128)(2,1)S(1)}, bf16[32,3584]{1,0:T(8,128)(2,1)S(1)}, u32[]{:S(2)}, u32[]{:S(2)}) collective-permute-start(bf16[32,3584]{1,0:T(8,128)(2,1)S(1)} %collective-permute-done.1), channel_id=1, source_target_pairs={{0,1},{1,2},{2,3},{3,0},{4,5},{5,6},{6,7},{7,4},{8,9},{9,10},{10,1... | collective-permute-start | bytes 688136 | tf_op jit(solution)/shard_map/ppermute | solution.py:107
  241.7 39.4 %collective-permute-start.3 = (bf16[4,128,4,512]{1,3,2,0:T(8,128)(2,1)}, bf16[4,128,4,512]{1,3,2,0:T(8,128)(2,1)}, u32[]{:S(2)}, u32[]{:S(2)}) collective-permute-start(bf16[4,128,4,512]{1,3,2,0:T(8,128)(2,1)} %pad_maximum_fusion), channel_id=1, source_target_pairs={{0,16},{1,17},{2,18},{3,19},{4,20},{5,21},{6,22},{7,23},{8,24},{9,... | collective-permute-start | bytes 6291464 | tf_op jit(solution)/shard_map/ppermute | solution.py:16
  254.7 83.0 %reduce-scatter.40.cloned.1.call-start = ((), (), s32[]{:S(2)}) async-start(), calls=%async_computation.20 | async-start | bytes 81920
  255.6 82.9 %reduce-scatter.36.cloned.1.call-start = ((), (), s32[]{:S(2)}) async-start(), calls=%async_computation.18 | async-start | bytes 81920
  256.5 82.7 %reduce-scatter.32.cloned.1.call-start = ((), (), s32[]{:S(2)}) async-start(), calls=%async_computation.16 | async-start | bytes 81920
  257.7 92.4 %reduce-scatter.42.cloned.1.call-start = ((), (), s32[]{:S(2)}) async-start(), calls=%async_computation.21 | async-start | bytes 81920
  285.6 84.1 %reduce-scatter.38.cloned.1.call-start = ((), (), s32[]{:S(2)}) async-start(), calls=%async_computation.19 | async-start | bytes 81920
  286.4 103.0 %reduce-scatter.34.cloned.1.call-start = ((), (), s32[]{:S(2)}) async-start(), calls=%async_computation.17 | async-start | bytes 81920
  287.2 121.7 %reduce-scatter.30.cloned.1.call-start = ((), (), s32[]{:S(2)}) async-start(), calls=%async_computation.15 | async-start | bytes 81920
  288.0 304.3 %reduce-scatter.26.cloned.1.call-start = ((), (), s32[]{:S(2)}) async-start(), calls=%async_computation.13 | async-start | bytes 33030144 | tf_op jit(solution)/shard_map/reduce_scatter | solution.py:164
  (22 other events, 179.8 us)
Sparse Core Ops, SparseCore 0:
  11.3 53.8 all-gather.6
  66.8 52.8 all-gather.8
  121.3 30.7 all-gather.10
  153.5 31.6 all-gather.4
  254.8 16.5 reduce-scatter.27
  273.5 17.4 reduce-scatter.39
  293.2 17.4 reduce-scatter.35
  312.9 17.4 reduce-scatter.31
  332.7 17.4 reduce-scatter.41
  352.2 17.4 reduce-scatter.37
  371.9 17.4 reduce-scatter.33
  391.5 17.4 reduce-scatter.29
  413.2 179.0 reduce-scatter.25
